TPU v7x, 256 devices: a whole 4x4x8 slice. The times are simulated.
256 devices in a mesh: copy: 2 (over core), shard: 16 (over y, x), cols: 8 (over z).
Axes of the slice: x: 4, y: 4, z: 8, core: 2. Of those that a mesh axis runs over, the one named last changes fastest.
Arguments:
- train_gate: float32 [5120, 9728], P(('copy', 'shard'), 'cols'), parts along dimension 0, may hold values from -0.15625 to 0.15625
- drift_gate: float32 [5120, 9728], P(('copy', 'shard'), 'cols'), parts along dimension 0, may hold values from -6 to 6
- spread_gate: float32 [5120, 9728], P(('copy', 'shard'), 'cols'), parts along dimension 0, may hold values from 0.1 to 10
- train_up: float32 [5120, 9728], P(('copy', 'shard'), 'cols'), parts along dimension 0, may hold values from -0.15625 to 0.15625
- drift_up: float32 [5120, 9728], P(('copy', 'shard'), 'cols'), parts along dimension 0, may hold values from -6 to 6
- spread_up: float32 [5120, 9728], P(('copy', 'shard'), 'cols'), parts along dimension 0, may hold values from 0.1 to 10
- norm_train: float32 [5120], P(('copy', 'shard', 'cols')), parts along dimension 0, may hold values from 0.25 to 1.75
- norm_step: float32 [5120], P(('copy', 'shard', 'cols')), parts along dimension 0, may hold values from -0.3 to 0.3
Outputs:
- final_gate: bfloat16 [5120, 9728], P('copy', 'cols'), parts along dimension 0
- final_up: bfloat16 [5120, 9728], P('copy', 'cols'), parts along dimension 0
- column_gate: float32 [19456], P(('copy', 'cols')), parts along dimension 0
- column_up: float32 [19456], P(('copy', 'cols')), parts along dimension 0
- serve_norm: bfloat16 [5120], P('copy'), parts along dimension 0
- result_gate: float32 [5120, 9728], P(('copy', 'shard'), 'cols'), parts along dimension 0
- result_up: float32 [5120, 9728], P(('copy', 'shard'), 'cols'), parts along dimension 0
There are 2 independent parts, one for each index of `copy`. A program takes and returns all parts, laid end to end along the dimension named above; each array names one. Nothing has to cross between parts.
All inputs are finite; a program needn't handle non-finite values.
Results may differ from a plain program's by a relative error of at most 0.0004.
Values may be sent and summed in bfloat16 or wider, within the bound.
A program may use at most 128 MiB of HBM per device.

v0:
```python
import jax
import jax.numpy as jnp
from jax import lax
from jax.sharding import Mesh
from jax.sharding import PartitionSpec as P

SHARD = ("shard_0", "shard_1")
SHARD_COLS = ("shard_0", "shard_1", "cols")
COPY_SHARD = ("copy", "shard_0", "shard_1")
COPY_SHARD_COLS = ("copy", "shard_0", "shard_1", "cols")


learn_rate = 0.015
decay_rate = 0.1
tiny_value = 1e-08


def sent_to_all(x, axis):
    length = lax.axis_size(axis)
    return lax.all_to_all(jnp.broadcast_to(x[None], (length, *x.shape)), axis, 0, 0, tiled=True)


def over_copies(x, axis):
    everything = sent_to_all(x, axis)
    return jnp.sum(everything, axis=0)


def packed_total(arrays, axis):
    ends = [0]
    for a in arrays:
        ends.append(ends[-1] + a.size)
    so_far = over_copies(jnp.concatenate([a.ravel() for a in arrays]), axis)
    return tuple((so_far[b:e].reshape(a.shape) for a, b, e in zip(arrays, ends, ends[1:])))


def in_one_piece(arrays, axis, dim, along):
    ends, at = ([], 0)
    for a in arrays[:-1]:
        at += a.shape[along]
        ends.append(at)
    both = jnp.concatenate(arrays, axis=along)
    return tuple(jnp.split(lax.all_gather(both, axis, axis=dim, tiled=True), ends, axis=along))


def laid_out(blocks, dim):
    blocks = jnp.moveaxis(blocks, 0, dim)
    lengths = blocks.shape
    return blocks.reshape(*lengths[:dim], lengths[dim] * lengths[dim + 1], *lengths[dim + 2 :])


def gather_in_order(x, axes, order):
    blocks = x
    for k in order:
        blocks = lax.all_gather(blocks, axes[k])
    done = order[::-1]
    back = [done.index(k) for k in range(len(axes))]
    blocks = blocks.transpose(*back, *range(len(axes), blocks.ndim))
    return blocks.reshape(-1, *x.shape)


def gather_axes(x, axes, order, dim):
    return laid_out(gather_in_order(x, axes, order), dim)


def local(
    train_gate, drift_gate, spread_gate, train_up, drift_up, spread_up, norm_train, norm_step
):
    result_gate = train_gate - learn_rate * (
        drift_gate / (jnp.sqrt(spread_gate) + tiny_value) + decay_rate * train_gate
    )
    result_up = train_up - learn_rate * (
        drift_up / (jnp.sqrt(spread_up) + tiny_value) + decay_rate * train_up
    )
    total_gate, total_up = packed_total(
        (jnp.sum(result_gate * result_gate, axis=0), jnp.sum(result_up * result_up, axis=0)), SHARD
    )
    column_gate = jnp.sqrt(total_gate)
    column_up = jnp.sqrt(total_up)
    narrow_gate, narrow_up = (
        (result_gate / column_gate).astype(jnp.bfloat16),
        (result_up / column_up).astype(jnp.bfloat16),
    )
    final_gate, final_up = in_one_piece((narrow_gate, narrow_up), SHARD, 0, 1)
    serve_norm = gather_axes(
        (norm_train + norm_step).astype(jnp.bfloat16), SHARD_COLS, (0, 1, 2), 0
    )
    return (final_gate, final_up, column_gate, column_up, serve_norm, result_gate, result_up)


def solution(mesh):
    finer = Mesh(
        mesh.devices.reshape(mesh.shape["copy"], 4, 4, mesh.shape["cols"]),
        ("copy", "shard_0", "shard_1", "cols"),
    )
    placed = (
        P(COPY_SHARD, "cols"),
        P(COPY_SHARD, "cols"),
        P(COPY_SHARD, "cols"),
        P(COPY_SHARD, "cols"),
        P(COPY_SHARD, "cols"),
        P(COPY_SHARD, "cols"),
        P(COPY_SHARD_COLS),
        P(COPY_SHARD_COLS),
    )
    return jax.shard_map(
        local,
        mesh=finer,
        in_specs=placed,
        out_specs=(
            P("copy", "cols"),
            P("copy", "cols"),
            P(("copy", "cols")),
            P(("copy", "cols")),
            P("copy"),
            P(COPY_SHARD, "cols"),
            P(COPY_SHARD, "cols"),
        ),
        check_vma=False,
    )
```

profile of v0, /device:TPU:32, one launch (start us, length us, event | category | flops | bytes accessed | tf_op | source)
XLA Modules:
  0.0 157.5 jit_solution(5735024962245769017)
XLA Ops:
  7.2 0.0 copy-start.6
  7.2 0.0 all-gather.6.cloned.1.call-start
  7.2 3.3 %multiply_reduce_fusion = (f32[1216]{0:T(1024)S(1)}, f32[160,1216]{1,0:T(8,128)S(1)}, f32[1216]{0:T(1024)S(1)}, f32[160,1216]{1,0:T(8,128)S(1)}) fusion(f32[160,1216]{1,0:T(8,128)} %param.11, f32[160,1216]{1,0:T(8,128)} %param.12, f32[160,1216]{1,0:T(8,128)} %param.13, f32[160,1216]{1,0:T(8,128)} %param.8, f32[160,1216]{1,0:T(8,128)} %param.9, ...), kind=kLoop, calls=%fused_computation.2 | loop fusion | flops 3110528 | bytes 6235648 | tf_op jit(solution)/shard_map/reduce_sum | solution.py:75
  10.5 0.0 copy-start
  10.5 0.1 pad_maximum_fusion.1
  10.6 0.1 broadcast_in_dim.2
  10.7 15.0 %all_to_all.6 = f32[16,1,2432]{2,1,0:T(1,128)S(1)} all-to-all(f32[16,1,2432]{2,1,0:T(1,128)S(1)} %broadcast_in_dim.2), channel_id=1, replica_groups=mesh['copy'=2,'shard_0'=4,'shard_1'=4,'cols'=8] {'shard_0','shard_1'}, dimensions={0} | all-to-all | bytes 311296 | tf_op jit(solution)/shard_map/all_to_all | solution.py:20
  25.7 0.1 reduce_sum.29
  25.8 0.1 slice_sqrt_fusion.1
  25.8 0.1 divide_convert_fusion.1
  25.9 0.1 divide_convert_fusion
  26.0 1.1 pad_maximum_fusion
  27.1 0.0 all-gather.6.cloned.1.call-update
  27.1 0.6 dynamic-slice
  28.4 0.2 dynamic-update-slice
  28.6 8.6 %all-reduce = bf16[80]{0:T(256)(128)(2,1)S(1)} all-reduce(bf16[80]{0:T(256)(128)(2,1)S(1)} %dynamic-update-slice), channel_id=2, replica_groups=mesh['copy'=2,'shard_0'=4,'shard_1'=4,'cols'=8] {'shard_0'}, use_global_device_ids=true, to_apply=%add | all-reduce | flops 80 | bytes 320
  37.2 0.1 reshape.28
  37.3 8.3 %all-gather.3 = bf16[4,4,20]{2,1,0:T(4,128)(2,1)S(1)} all-gather(bf16[1,4,20]{2,1,0:T(4,128)(2,1)S(1)} %reshape.28), channel_id=3, replica_groups=mesh['copy'=2,'shard_0'=4,'shard_1'=4,'cols'=8] {'shard_1'}, dimensions={0}, use_global_device_ids=true | all-gather | bytes 800 | tf_op jit(solution)/shard_map/all_gather | solution.py:54
  45.6 27.5 %all-gather.2 = bf16[32,4,20]{2,1,0:T(4,128)(2,1)S(1)} all-gather(bf16[4,4,20]{2,1,0:T(4,128)(2,1)S(1)} %all-gather.3), channel_id=4, replica_groups=mesh['copy'=2,'shard_0'=4,'shard_1'=4,'cols'=8] {'cols'}, dimensions={0}, use_global_device_ids=true | all-gather | bytes 5760 | tf_op jit(solution)/shard_map/all_gather | solution.py:54
  73.0 0.7 reshape_reshape.3
  73.7 46.5 %all-gather.6.cloned.1.call-done = bf16[2560,2432]{1,0:T(8,128)(2,1)} async-done(((bf16[160,2432]{1,0:T(8,128)(2,1)}), bf16[2560,2432]{1,0:T(8,128)(2,1)}) %all-gather.6.cloned.1.call-update) | async-done | bytes 12451856 | tf_op jit(solution)/shard_map/all_gather | solution.py:42
  120.2 11.8 %fusion = (bf16[2560,1216]{1,0:T(8,128)(2,1)}, bf16[2560,1216]{1,0:T(8,128)(2,1)}) fusion(bf16[2560,2432]{1,0:T(8,128)(2,1)} %all-gather.6.cloned.1.call-done), kind=kLoop, calls=%fused_computation.12 | loop fusion | bytes 24903680 | tf_op jit(solution)/shard_map/split | solution.py:42
  132.0 9.3 %copy.28 = bf16[2560,1216]{0,1:T(8,128)(2,1)} copy(bf16[2560,1216]{1,0:T(8,128)(2,1)} %get-tuple-element.47) | data formatting | bytes 12451840
  141.4 9.3 %copy.29 = bf16[2560,1216]{0,1:T(8,128)(2,1)} copy(bf16[2560,1216]{1,0:T(8,128)(2,1)} %get-tuple-element.46) | data formatting | bytes 12451840
  (15 shorter events, 0.0 us)
Async XLA Ops:
  7.2 19.9 %copy-start.6 = (u32[256]{0:T(256)S(1)}, u32[256]{0:T(256)}, u32[]{:S(2)}) copy-start(u32[256]{0:T(256)} %constant.12) | copy-start | bytes 3076
  7.2 21.2 %copy-start.4 = (f32[20]{0:T(128)S(1)}, f32[20]{0:T(128)}, u32[]{:S(2)}) copy-start(f32[20]{0:T(128)} %param.14) | copy-start | bytes 244
  7.2 21.2 %copy-start.5 = (f32[20]{0:T(128)S(1)}, f32[20]{0:T(128)}, u32[]{:S(2)}) copy-start(f32[20]{0:T(128)} %param.15) | copy-start | bytes 244
  7.2 113.0 %all-gather.6.cloned.1.call-start = ((), (), s32[]{:S(2)}) async-start(), calls=%async_computation.1 | async-start | bytes 13230080 | tf_op jit(solution)/shard_map/all_gather | solution.py:42
  10.5 121.5 %copy-start = (f32[160,1216]{1,0:T(8,128)}, f32[160,1216]{1,0:T(8,128)S(1)}, u32[]{:S(2)}) copy-start(f32[160,1216]{1,0:T(8,128)S(1)} %get-tuple-element.45) | copy-start | bytes 2334724
  10.5 121.5 %copy-start.1 = (f32[160,1216]{1,0:T(8,128)}, f32[160,1216]{1,0:T(8,128)S(1)}, u32[]{:S(2)}) copy-start(f32[160,1216]{1,0:T(8,128)S(1)} %get-tuple-element.51) | copy-start | bytes 2334724
  25.8 106.2 %copy-start.2 = (f32[1216]{0:T(1024)}, f32[1216]{0:T(1024)S(1)}, u32[]{:S(2)}) copy-start(f32[1216]{0:T(1024)S(1)} %get-tuple-element.48) | copy-start | bytes 14596
  25.8 106.2 %copy-start.3 = (f32[1216]{0:T(1024)}, f32[1216]{0:T(1024)S(1)}, u32[]{:S(2)}) copy-start(f32[1216]{0:T(1024)S(1)} %get-tuple-element.49) | copy-start | bytes 14596
Sparse Core Ops, SparseCore 0:
  27.2 92.9 all-gather.5
where the time goes:
time: 159 us; the launch traced here: 158 us
  blocking collectives  59.3 us (37%)
  waiting for transfers between devices  46.5 us (29%)
  local copies, waits for them, and re-layouts  32.3 us (20%)
  between operations  14.8 us (9%)
  other arithmetic  4.64 us (3%)
    all_gather x1, waiting for transfers between devices, in_one_piece(): lax.all_gather(both, axis, axis=dim, tiled=True)  46.5 us
    all_gather x2, blocking collectives, gather_in_order(): blocks = lax.all_gather(blocks, axes[k])  35.7 us
    unnamed x20, local copies, waits for them, and re-layouts  19.6 us
    all_to_all x1, blocking collectives, sent_to_all(): lax.all_to_all(jnp.broadcast_to(x[None], (length, *x.shape)), axis, 0, 0,...  15 us
    split x1, local copies, waits for them, and re-layouts, in_one_piece(): jnp.split(lax.all_gather(both, axis, axis=dim, tiled=True), ends, axis=al...  11.8 us
    unnamed x1, blocking collectives  8.56 us
    reduce_sum x1, other arithmetic, local(): jnp.sum(result_up * result_up, axis=0)  3.26 us
  transfers between devices with their start and end apart: 1, of which 1 were waited for; matrix products, arithmetic and copies ran while one was open for 1% of the time, Pallas kernels for 0%

commit v1 on v0

v1 whole, which is shorter than its diff:
```python
import jax
import jax.numpy as jnp
from jax import lax
from jax.experimental import pallas as pl
from jax.experimental.pallas import tpu as pltpu
from jax.sharding import Mesh
from jax.sharding import PartitionSpec as P

MESH = pl.DeviceIdType.MESH
AXES = ("copy", "shard_0", "shard_1", "cols")
Y, X, Z = "shard_0", "shard_1", "cols"
N = 4

learn_rate = 0.015
decay_rate = 0.1
tiny_value = 1e-08

F32, BF16 = jnp.float32, jnp.bfloat16
ROWS, COLS, LANES = 160, 1216, 128
FULL = COLS // LANES
BLOCKS = 2 * FULL + 1
TAIL = COLS - FULL * LANES
FIRST = 8
PAIRS = FULL + 1


def updated(t, d, s):
    return t - learn_rate * (d / (jnp.sqrt(s) + tiny_value) + decay_rate * t)


def pieces(start, length):
    while length:
        here = min(length, LANES - start % LANES)
        yield start // LANES, start % LANES, here
        start, length = start + here, length - here


def unit_of(pair, along_x):
    if pair < FULL:
        return 2 * pair + (0 if along_x else 1), 0, ROWS
    return BLOCKS - 1, (0 if along_x else ROWS // 2), ROWS // 2


def gather_kernel(
    tg, dg, sg, tu, du, su, nt, ns,
    g, rg, ru, cg, cu, norm,
    tgv, dgv, sgv, tuv, duv, suv, ntv, nsv, stats, scale, n1, n2, dense,
    in_sem, stat_send, stat_recv, z_send, z_recv, n_send, n_recv, send, recv,
):
    x, y, z = lax.axis_index(X), lax.axis_index(Y), lax.axis_index(Z)
    me = y * N + x
    depth = n1.shape[0]
    right, left = lax.rem(x + 1, N), lax.rem(x + N - 1, N)
    up, down = lax.rem(y + 1, N), lax.rem(y + N - 1, N)

    loads = [
        pltpu.make_async_copy(a, b, in_sem.at[i])
        for i, (a, b) in enumerate(
            ((tg, tgv), (dg, dgv), (sg, sgv), (tu, tuv), (du, duv), (su, suv), (nt, ntv), (ns, nsv))
        )
    ]
    for load in loads:
        load.start()

    peers = [
        (k, {Y: lax.rem(y + k // N, N), X: lax.rem(x + k % N, N)}) for k in range(1, N * N)
    ]
    deep = [(k, {Z: lax.rem(z + k, depth)}) for k in range(1, depth)]
    barrier = pltpu.get_barrier_semaphore()
    for _, peer in peers + deep:
        pl.semaphore_signal(barrier, inc=1, device_id=peer, device_id_type=MESH)

    def remote(src, dst, s, r, peer):
        return pltpu.make_async_remote_copy(
            src_ref=src, dst_ref=dst, send_sem=s, recv_sem=r, device_id=peer, device_id_type=MESH
        )

    def sums_of(c, src, out):
        t, d, s = src
        lanes = pl.ds(pl.multiple_of(c * LANES, LANES), LANES)
        total = jnp.zeros((8, LANES), F32)
        for r in range(0, ROWS, 8):
            v = updated(t[pl.ds(r, 8), lanes], d[pl.ds(r, 8), lanes], s[pl.ds(r, 8), lanes])
            out[pl.ds(r, 8), lanes] = v
            total = total + v * v
        return jnp.sum(total, axis=0, keepdims=True)

    gate, upper = (tgv, dgv, sgv), (tuv, duv, suv)
    for load in loads[:3]:
        load.wait()
    for c in range(FIRST):
        stats[me, pl.ds(c, 1), :] = sums_of(c, gate, rg)

    def stat_copies(part, first, rows):
        return [
            remote(
                stats.at[me, pl.ds(first, rows)], stats.at[me, pl.ds(first, rows)],
                stat_send.at[part, k], stat_recv.at[part, k], peer,
            )
            for k, peer in peers
        ]

    pl.semaphore_wait(barrier, N * N - 1 + depth - 1)
    stats_a = stat_copies(0, 0, FIRST)
    for copy in stats_a:
        copy.start()

    for load in loads[3:]:
        load.wait()
    for c in range(FIRST, FULL):
        stats[me, pl.ds(c, 1), :] = sums_of(c, gate, rg)
    for c in range(FULL):
        stats[me, pl.ds(FULL + c, 1), :] = sums_of(c, upper, ru)
    tail = pl.ds(FULL * LANES, TAIL)
    tails = []
    for (t, d, s), out in ((gate, rg), (upper, ru)):
        v = updated(t[:, tail], d[:, tail], s[:, tail])
        out[:, tail] = v
        tails.append(v)
    mixed = jnp.concatenate(tails, axis=1)
    stats[me, pl.ds(BLOCKS - 1, 1), :] = jnp.sum(mixed * mixed, axis=0, keepdims=True)
    stats[me, pl.ds(BLOCKS, 24 - BLOCKS), :] = jnp.zeros((24 - BLOCKS, LANES), F32)
    stats_b = stat_copies(1, FIRST, 24 - FIRST)
    for copy in stats_b:
        copy.start()

    n1[z] = jnp.zeros((8, LANES), F32)
    n1[z, pl.ds(0, 1), pl.ds(0, 20)] = ntv[...] + nsv[...]
    over_z = [remote(n1.at[z], n1.at[z], z_send.at[k], z_recv.at[k], peer) for k, peer in deep]
    for copy in over_z:
        copy.start()

    def part_of(unit, first_row, rows, ys, xs):
        return g.at[unit, ys, xs, pl.ds(first_row, rows)]

    one = lambda i: pl.ds(i, 1)
    every = pl.ds(0, N)

    def hop(stage, pair, along_x, forward):
        c, r0, rows = unit_of(pair, along_x)
        on_x = along_x == (stage < 2)
        if on_x:
            peer = {X: right if forward else left}
            source = left if forward else right
        else:
            peer = {Y: up if forward else down}
            source = down if forward else up
        if stage == 0:
            ref = part_of(c, r0, rows, one(y), one(x))
        elif stage == 1:
            half = rows // 2
            r = r0 if forward else r0 + half
            ref = part_of(c, r, half, *((one(y), one(source)) if on_x else (one(source), one(x))))
        elif stage == 2:
            ref = part_of(c, r0, rows, *((every, one(x)) if on_x else (one(y), every)))
        else:
            half = pl.ds(0 if forward else N // 2, N // 2)
            ref = part_of(c, r0, rows, *((half, one(source)) if on_x else (one(source), half)))
        kind = (0 if along_x else 2) + (0 if forward else 1)
        return remote(ref, ref, send.at[stage, kind], recv.at[stage, pair, kind], peer)

    WAYS = [(a, f) for a in (True, False) for f in (True, False)]

    def start(stage, pair):
        for along_x, forward in WAYS:
            hop(stage, pair, along_x, forward).start()

    def arrived(stage, pair):
        for along_x, forward in WAYS:
            hop(stage, pair, along_x, forward).wait_recv()

    def take_scale(copies, first, rows):
        for copy in copies:
            copy.wait_recv()
        total = stats[0, pl.ds(first, rows), :]
        for p in range(1, N * N):
            total = total + stats[p, pl.ds(first, rows), :]
        scale[pl.ds(first, rows), :] = jnp.sqrt(total)

    def put(c):
        by = scale[pl.ds(c, 1), :]
        if c < BLOCKS - 1:
            src, at = (rg, c) if c < FULL else (ru, c - FULL)
            v = src[:, pl.ds(at * LANES, LANES)]
        else:
            v = jnp.concatenate([rg[:, tail], ru[:, tail]], axis=1)
        g[c, y, x] = (v / by).astype(BF16)

    take_scale(stats_a, 0, FIRST)
    for pair in range(FIRST // 2):
        put(2 * pair)
        put(2 * pair + 1)
        start(0, pair)
    take_scale(stats_b, FIRST, 24 - FIRST)
    for pair in range(FIRST // 2, PAIRS):
        put(2 * pair)
        if pair < FULL:
            put(2 * pair + 1)
        start(0, pair)

    for out, base, lane in ((cg, 0, 0), (cu, FULL, TAIL)):
        out[pl.ds(0, FULL), :] = scale[pl.ds(base, FULL), :]
        out[pl.ds(FULL, 1), pl.ds(0, TAIL)] = scale[pl.ds(BLOCKS - 1, 1), pl.ds(lane, TAIL)]

    for pair in range(PAIRS):
        arrived(0, pair)
        start(1, pair)

    for copy in over_z:
        copy.wait_recv()
    n2[me] = jnp.zeros((8, LANES), F32)
    for k in range(depth):
        done = 0
        for row, lane, length in pieces(20 * k, 20):
            n2[me, pl.ds(row, 1), pl.ds(lane, length)] = n1[k, pl.ds(0, 1), pl.ds(done, length)]
            done += length
    over_plane = [remote(n2.at[me], n2.at[me], n_send.at[k], n_recv.at[k], peer) for k, peer in peers]
    for copy in over_plane:
        copy.start()

    for pair in range(PAIRS + 1):
        if pair < PAIRS:
            arrived(1, pair)
            start(2, pair)
        if pair:
            arrived(2, pair - 1)
            start(3, pair - 1)

    for copy in over_plane:
        copy.wait_recv()
    for p in range(N * N):
        for row, lane, length in pieces(0, ROWS):
            done = 0
            for to_row, to_lane, part in pieces(ROWS * p + row * LANES, length):
                dense[pl.ds(to_row, 1), pl.ds(to_lane, part)] = n2[p, pl.ds(row, 1), pl.ds(done, part)]
                done += part
    norm[...] = dense[...].astype(BF16)

    for pair in range(PAIRS):
        arrived(3, pair)

    for copy in stats_a + stats_b + over_z + over_plane:
        copy.wait_send()
    for stage in range(4):
        half = pl.ds(0, ROWS // 2 if stage != 1 else ROWS // 4)
        xs = pl.ds(0, (1, 1, N, N // 2)[stage])
        sent = g.at[:, 0, xs, half]
        for along_x, forward in WAYS:
            kind = (0 if along_x else 2) + (0 if forward else 1)
            remote(sent, sent, send.at[stage, kind], recv.at[stage, 0, kind], {X: right}).wait_send()


def write_kernel(
    g, rg, ru, cg_in, cu_in, norm_in, fg, fu, og, ou, cg, cu, norm, tiles, out_sem, tile_sem
):
    others = [
        pltpu.make_async_copy(a, b, out_sem.at[i])
        for i, (a, b) in enumerate(
            ((rg, og), (ru, ou), (cg_in, cg), (cu_in, cu), (norm_in, norm))
        )
    ]
    for copy in others:
        copy.start()
    slots = tiles.shape[0]
    rows = N * ROWS

    def turn(c, slot):
        for s in range(N):
            block = g[c, s].reshape(rows, LANES)
            tiles[slot, :, pl.ds(s * rows, rows)] = block.T

    def sweep(base, out):
        def step(i, _):
            slot = lax.rem(i, slots)
            dst = out.at[pl.ds(pl.multiple_of(i * LANES, LANES), LANES)]
            copy = pltpu.make_async_copy(tiles.at[slot], dst, tile_sem.at[slot])

            @pl.when(i >= slots)
            def _():
                copy.wait()

            turn(base + i, slot)
            copy.start()
            return 0

        lax.fori_loop(0, FULL, step, 0)
        for i in range(FULL - slots, FULL):
            pltpu.make_async_copy(
                tiles.at[i % slots], out.at[pl.ds(i * LANES, LANES)], tile_sem.at[i % slots]
            ).wait()

    sweep(0, fg)
    sweep(FULL, fu)
    turn(BLOCKS - 1, 0)
    ends = [
        pltpu.make_async_copy(
            tiles.at[0, pl.ds(TAIL * i, TAIL)], out.at[pl.ds(FULL * LANES, TAIL)], tile_sem.at[i]
        )
        for i, out in enumerate((fg, fu))
    ]
    for copy in ends:
        copy.start()
    for copy in ends + others:
        copy.wait()


def local(train_gate, drift_gate, spread_gate, train_up, drift_up, spread_up, norm_train, norm_step):
    arrays = (train_gate, drift_gate, spread_gate, train_up, drift_up, spread_up)
    arrays += (norm_train.reshape(1, 20), norm_step.reshape(1, 20))
    depth = lax.axis_size(Z)
    wide = (ROWS, COLS)
    dma = pltpu.SemaphoreType.DMA
    g, rg, ru, cg, cu, norm = pl.pallas_call(
        gather_kernel,
        out_shape=(
            pltpu.VMEM((BLOCKS, N, N, ROWS, LANES), BF16),
            pltpu.VMEM(wide, F32),
            pltpu.VMEM(wide, F32),
            pltpu.VMEM((FULL + 1, LANES), F32),
            pltpu.VMEM((FULL + 1, LANES), F32),
            pltpu.VMEM((20, LANES), BF16),
        ),
        in_specs=[pl.BlockSpec(memory_space=pltpu.HBM)] * 8,
        out_specs=(pl.BlockSpec(memory_space=pltpu.VMEM),) * 6,
        scratch_shapes=[pltpu.VMEM(wide, F32)] * 6
        + [pltpu.VMEM((1, 20), F32)] * 2
        + [
            pltpu.VMEM((N * N, 24, LANES), F32),
            pltpu.VMEM((24, LANES), F32),
            pltpu.VMEM((depth, 8, LANES), F32),
            pltpu.VMEM((N * N, 8, LANES), F32),
            pltpu.VMEM((20, LANES), F32),
            dma((8,)),
            dma((2, N * N)),
            dma((2, N * N)),
            dma((depth,)),
            dma((depth,)),
            dma((N * N,)),
            dma((N * N,)),
            dma((4, 4)),
            dma((4, PAIRS, 4)),
        ],
        compiler_params=pltpu.CompilerParams(
            collective_id=0, has_side_effects=True, vmem_limit_bytes=24 * 2**20
        ),
        name="update_and_gather",
    )(*(pltpu.with_memory_space_constraint(a, pltpu.HBM) for a in arrays))
    turned = (COLS, N * N * ROWS)
    fg, fu, og, ou, cg, cu, serve = pl.pallas_call(
        write_kernel,
        out_shape=(jax.ShapeDtypeStruct(turned, BF16),) * 2
        + (jax.ShapeDtypeStruct(wide, F32),) * 2
        + (jax.ShapeDtypeStruct((FULL + 1, LANES), F32),) * 2
        + (jax.ShapeDtypeStruct((20, LANES), BF16),),
        in_specs=[pl.BlockSpec(memory_space=pltpu.VMEM)] * 6,
        out_specs=(pl.BlockSpec(memory_space=pltpu.HBM),) * 7,
        scratch_shapes=[pltpu.VMEM((4, LANES, N * N * ROWS), BF16), dma((5,)), dma((4,))],
        compiler_params=pltpu.CompilerParams(vmem_limit_bytes=16 * 2**20),
        name="turn_and_write",
    )(g, rg, ru, cg, cu, norm)
    return (
        fg.T, fu.T, cg.reshape(-1)[:COLS], cu.reshape(-1)[:COLS], serve.reshape(-1), og, ou,
    )


def solution(mesh):
    finer = Mesh(
        mesh.devices.reshape(mesh.shape["copy"], N, N, mesh.shape["cols"]), AXES
    )
    held = P(("copy", Y, X), Z)
    return jax.shard_map(
        local,
        mesh=finer,
        in_specs=(held,) * 6 + (P(AXES),) * 2,
        out_specs=(P("copy", Z), P("copy", Z), P(("copy", Z)), P(("copy", Z)), P("copy"), held, held),
        check_vma=False,
    )
```

time: 159 us -> 92.2 us (0.58)
  Pallas kernels: 0 us -> 91.5 us
  blocking collectives: 59.3 us -> 0 us
  waiting for transfers between devices: 46.5 us -> 0 us
  local copies, waits for them, and re-layouts: 32.3 us -> 0 us
  between operations: 14.8 us -> 0.64 us
  other arithmetic: 4.64 us -> 0 us
    pallas_call x0 -> x2, Pallas kernels: none -> 91.5 us  [the longest x1 83.6 us: local(): pl.pallas_call(gather_kernel, out_shape=(pltpu.VMEM((BLOCKS, N, N, ROWS,...]
    all_gather x1 -> x0, waiting for transfers between devices: 46.5 us -> none  [in_one_piece(): lax.all_gather(both, axis, axis=dim, tiled=True)]
    all_gather x2 -> x0, blocking collectives: 35.7 us -> none  [gather_in_order(): blocks = lax.all_gather(blocks, axes[k])]
    unnamed x20 -> x0, local copies, waits for them, and re-layouts: 19.6 us -> none
    all_to_all x1 -> x0, blocking collectives: 15 us -> none  [sent_to_all(): lax.all_to_all(jnp.broadcast_to(x[None], (length, *x.shape)), axis, 0, 0,...]
    split x1 -> x0, local copies, waits for them, and re-layouts: 11.8 us -> none  [in_one_piece(): jnp.split(lax.all_gather(both, axis, axis=dim, tiled=True), ends, axis=al...]
    unnamed x1 -> x0, blocking collectives: 8.56 us -> none
    reduce_sum x2 -> x0, other arithmetic: 3.36 us -> none  [the longest x1 3.26 us: local(): jnp.sum(result_up * result_up, axis=0)]
  transfers between devices with their start and end apart: 1 -> 0, of which waited for: 1 -> 0; matrix products, arithmetic and copies ran while one was open for 1% -> 0% of each run, Pallas kernels for 0% -> 0%
where the time goes in v1:
time: 92.2 us; the launch traced here: 92.1 us
  Pallas kernels  91.5 us (99%)
    pallas_call x1, Pallas kernels, local(): pl.pallas_call(gather_kernel, out_shape=(pltpu.VMEM((BLOCKS, N, N, ROWS,...  83.6 us
    pallas_call x1, Pallas kernels, local(): pl.pallas_call(write_kernel, out_shape=(jax.ShapeDtypeStruct(turned, BF16...  7.82 us

profile of v1, /device:TPU:32, one launch (start us, length us, event | category | flops | bytes accessed | tf_op | source)
XLA Modules:
  0.0 92.1 jit_solution(11531141030783441969)
XLA Ops:
  0.6 83.6 %update_and_gather.1 = (bf16[19,4,4,160,128]{4,3,2,1,0:T(8,128)(2,1)S(1)}, f32[160,1216]{1,0:T(8,128)S(1)}, f32[160,1216]{1,0:T(8,128)S(1)}, f32[10,128]{1,0:T(8...) custom-call(f32[160,1216]{1,0:T(8,128)} %tg.1, f32[160,1216]{1,0:T(8,128)} %dg.1, f32[160,1216]{1,0:T(8,128)} %sg.1, ...), custom_call_target="tpu_custom_call" | custom-call | tf_op jit(solution)/shard_map/update_and_gather/pallas_call | solution.py:313
  84.3 7.8 %turn_and_write.1 = (bf16[1216,2560]{1,0:T(8,128)(2,1)}, bf16[1216,2560]{1,0:T(8,128)(2,1)}, f32[160,1216]{1,0:T(8,128)}, f32[160,1216]{1,0:T(8,128)}, f32[10,12...) custom-call(bf16[19,4,4,160,128]{4,3,2,1,0:T(8,128)(2,1)S(1)} %get-tuple-element.20.g, ...), custom_call_target="tpu_custom_call" | custom-call | tf_op jit(solution)/shard_map/turn_and_write/pallas_call | solution.py:349
